TPU v7x, 256 devices: a 8x8x2 block of a 8x8x16 slice. The times are simulated.
256 devices in a mesh: grp: 2 (over z), seq: 128 (over y, x, core).
Axes of the slice: x: 8, y: 8, z: 2, core: 2. Of those that a mesh axis runs over, the one named last changes fastest.
The devices are a block of a 8x8x16 slice.
Arguments:
- queries: bfloat16 [256, 4096], P(('grp', 'seq')), parts along dimension 0, may hold values from -9 to 9
- question_keys: bfloat16 [256, 2048], P(('grp', 'seq')), parts along dimension 0, may hold values from -4 to 4
- question_values: bfloat16 [256, 2048], P(('grp', 'seq')), parts along dimension 0, may hold values from -5 to 5
- doc_keys: bfloat16 [131072, 2048], P(('grp', 'seq')), parts along dimension 0, may hold values from -4 to 4
- doc_values: bfloat16 [131072, 2048], P(('grp', 'seq')), parts along dimension 0, may hold values from -5 to 5
- lengths: int32 [2], P('grp'), parts along dimension 0, may hold values from 4 to 128
- offsets: int32 [2], P('grp'), parts along dimension 0, may hold values from 2 to 65536, as said below
Outputs:
- attended: bfloat16 [256, 4096], P(('grp', 'seq')), parts along dimension 0
There are 2 independent parts, one for each index of `grp`. A program takes and returns all parts, laid end to end along the dimension named above; each array names one. Nothing has to cross between parts.
Inputs may be any that keep to these rules, and one draw needn't show every extreme that they name: Some question has offsets equal to 65536.
All inputs are finite; a program needn't handle non-finite values.
Results may differ from a plain program's by a relative error of at most 0.0029.
Values may be sent and summed in bfloat16 or wider, within the bound.
A program may use at most 64 MiB of HBM per device.

v0:
```python
import math

import jax
import jax.numpy as jnp
from jax import lax
from jax.sharding import Mesh
from jax.sharding import PartitionSpec as P

H = 32
KVH = 16
HD = 128
QSCALE = 144
QL = 128
NQ = 1
SEQ = ("seq_0", "seq_1", "seq_2")
GRP_SEQ = ("grp", "seq_0", "seq_1", "seq_2")


MASKED = -1e30


def laid_out(tiles, dim):
    lengths = list(tiles.shape[1:])
    lengths[dim] *= tiles.shape[0]
    return jnp.moveaxis(tiles, 0, dim).reshape(lengths)


def stacked_from(array, axes, turns):
    tiles = array
    for k in turns:
        tiles = lax.all_gather(tiles, axes[k])
    done = turns[::-1]
    back = [done.index(k) for k in range(len(axes))]
    tiles = tiles.transpose(*back, *range(len(axes), tiles.ndim))
    return tiles.reshape(-1, *array.shape)


def gather_axes(array, axes, turns, dim):
    return laid_out(stacked_from(array, axes, turns), dim)


def side_by_side(arrays, axis, split_dim, concat_dim, along):
    both = jnp.concatenate(arrays, axis=along)
    whole, at, done = (
        lax.all_to_all(both, axis, split_axis=split_dim, concat_axis=concat_dim, tiled=True),
        0,
        [],
    )
    for a in arrays:
        done.append(lax.slice_in_dim(whole, at, at + a.shape[along], axis=along))
        at += a.shape[along]
    return tuple(done)


def row_tables(start, count, lengths, offsets):
    rows = start + jnp.arange(count, dtype=jnp.int32)
    question = rows // QL
    position = rows % QL
    owner_table = question[:, None] == jnp.arange(NQ, dtype=jnp.int32)[None, :]
    row_length = jnp.sum(jnp.where(owner_table, lengths[None, :], 0), axis=1)
    row_offset = jnp.sum(jnp.where(owner_table, offsets[None, :], 0), axis=1)
    return (question, position, position < row_length, row_offset)


def local(queries, question_keys, question_values, doc_keys, doc_values, lengths, offsets):
    rows_local = queries.shape[0]
    doc_local = doc_keys.shape[0]
    device_count = lax.axis_size(SEQ)
    device_index = lax.axis_index(SEQ)
    total_rows = rows_local * device_count
    per_group = H // KVH
    factor_q = QSCALE ** (-0.5)
    key_doc = doc_keys.reshape(doc_local, KVH, HD)
    value_doc = doc_values.reshape(doc_local, KVH, HD)
    key_self = question_keys.reshape(rows_local, KVH, HD)
    value_self = question_values.reshape(rows_local, KVH, HD)
    doc_places = device_index * doc_local + jnp.arange(doc_local, dtype=jnp.int32)
    self_rows = device_index * rows_local + jnp.arange(rows_local, dtype=jnp.int32)
    whole = gather_axes(queries, (("seq_0", "seq_1"), "seq_2"), (0, 1), 0)
    block_rows = math.gcd(total_rows, 512)
    block_count = total_rows // block_rows

    def one_block(start):
        piece = whole.reshape(block_rows, KVH, per_group, HD)
        question, position, live_rows, row_offset = row_tables(start, block_rows, lengths, offsets)
        mask_doc = live_rows[:, None] & (doc_places[None, :] < row_offset[:, None])
        mask_self = (
            live_rows[:, None]
            & (self_rows[None, :] // QL == question[:, None])
            & (self_rows[None, :] % QL <= position[:, None])
        )
        mask_doc = mask_doc[:, None, None, :]
        mask_self = mask_self[:, None, None, :]
        scores_doc = (
            jnp.einsum("rgjd,kgd->rgjk", piece, key_doc, preferred_element_type=jnp.float32)
            * factor_q
        )
        scores_self = (
            jnp.einsum("rgjd,kgd->rgjk", piece, key_self, preferred_element_type=jnp.float32)
            * factor_q
        )
        scores_doc = jnp.where(mask_doc, scores_doc, MASKED)
        scores_self = jnp.where(mask_self, scores_self, MASKED)
        block_top = jnp.maximum(jnp.max(scores_doc, axis=-1), jnp.max(scores_self, axis=-1))
        weights_doc = jnp.where(mask_doc, jnp.exp(scores_doc - block_top[..., None]), 0.0).astype(
            jnp.bfloat16
        )
        weights_self = jnp.where(
            mask_self, jnp.exp(scores_self - block_top[..., None]), 0.0
        ).astype(jnp.bfloat16)
        block_den = jnp.sum(weights_doc.astype(jnp.float32), axis=-1) + jnp.sum(
            weights_self.astype(jnp.float32), axis=-1
        )
        block_num = jnp.einsum(
            "rgjk,kgd->rgjd", weights_doc, value_doc, preferred_element_type=jnp.float32
        )
        block_num = block_num + jnp.einsum(
            "rgjk,kgd->rgjd", weights_self, value_self, preferred_element_type=jnp.float32
        )
        return (
            block_num.reshape(block_rows, H * HD),
            block_top.reshape(block_rows, H),
            block_den.reshape(block_rows, H),
        )

    starts = jnp.arange(block_count, dtype=jnp.int32) * block_rows
    numer, row_top, denom = lax.map(one_block, starts)
    numer = numer.reshape(total_rows, H * HD)
    row_top = row_top.reshape(total_rows, H)
    denom = denom.reshape(total_rows, H)
    got_num, got_top, got_den = side_by_side(
        (numer[None], row_top[None], denom[None]), SEQ, 1, 0, 2
    )
    overall = jnp.max(got_top, axis=0)
    rescale = jnp.exp(got_top - overall[None])
    total_num = jnp.sum(
        got_num.reshape(device_count, rows_local, H, HD) * rescale[:, :, :, None], axis=0
    )
    total_den = jnp.sum(got_den * rescale, axis=0)
    question, position, live_rows, row_offset = row_tables(
        device_index * rows_local, rows_local, lengths, offsets
    )
    safe_den = jnp.where(live_rows[:, None], total_den, 1.0)
    result = (total_num / safe_den[:, :, None]).reshape(rows_local, H * HD)
    return jnp.where(live_rows[:, None], result, 0.0).astype(jnp.bfloat16)


def solution(mesh):
    torus = Mesh(
        mesh.devices.reshape(mesh.shape["grp"], 8, 8, 2), ("grp", "seq_0", "seq_1", "seq_2")
    )
    return jax.shard_map(
        local,
        mesh=torus,
        in_specs=(
            P(GRP_SEQ, None),
            P(GRP_SEQ, None),
            P(GRP_SEQ, None),
            P(GRP_SEQ, None),
            P(GRP_SEQ, None),
            P("grp"),
            P("grp"),
        ),
        out_specs=P(GRP_SEQ, None),
        check_vma=False,
    )
```

profile of v0, /device:TPU:513, one launch (start us, length us, event | category | flops | bytes accessed | tf_op | source)
XLA Modules:
  0.0 204.3 jit_solution(15102384464502453705)
XLA Ops:
  6.5 0.0 copy-start.1
  6.5 0.0 all-gather.5.cloned.1.call-start
  6.6 49.6 %all-gather.2 = bf16[64,1,4096]{2,1,0:T(2,128)(2,1)S(1)} all-gather(bf16[1,1,4096]{2,1,0:T(2,128)(2,1)} %bitcast.107), channel_id=2, replica_groups=mesh['grp'=2,'seq_0'=8,'seq_1'=8,'seq_2'=2] {'seq_0','seq_1'}, dimensions={0}, use_global_device_ids=true | all-gather | bytes 532480 | tf_op jit(solution)/shard_map/all_gather | solution.py:31
  56.2 1.4 copy.61
  57.5 0.1 all-gather.5.cloned.1.call-update
  58.9 0.0 copy-done.1
  58.9 2.0 copy.48
  60.9 0.0 copy-start.3
  60.9 0.0 copy-start.4
  60.9 3.9 %copy.45 = bf16[512,2048]{0,1:T(8,128)(2,1)} copy(bf16[512,2048]{1,0:T(8,128)(2,1)} %param.11) | data formatting | bytes 4194304 | tf_op jit(solution)/shard_map/reshape | solution.py:74
  64.8 0.0 copy-done.3
  64.9 0.0 copy-done.4
  65.0 0.1 compare_and_fusion
  65.1 27.4 %all-gather.5.cloned.1.call-done = bf16[128,4096]{1,0:T(8,128)(2,1)} async-done(((bf16[64,4096]{1,0:T(8,128)(2,1)}), bf16[128,4096]{1,0:T(8,128)(2,1)}) %all-gather.5.cloned.1.call-update) | async-done | bytes 1048592 | tf_op jit(solution)/shard_map/all_gather | solution.py:31
  92.5 2.3 %copy.60 = bf16[2,64,1,4096]{3,0,1,2:T(2,128)(2,1)S(1)} copy(bf16[2,64,1,4096]{3,1,0,2:T(8,128)(2,1)} %bitcast.98) | data formatting | bytes 2097152 | tf_op jit(solution)/shard_map/all_gather | solution.py:31
  94.8 0.8 reshape_reshape_reshape.4
  95.7 2.3 %multiply_reduce_fusion = f32[16,128,2]{2,0,1:T(8,128)S(1)} fusion(f32[16,128]{1,0:T(8,128)S(1)} %bitcast_convert_fusion, bf16[128,16,2,128]{3,2,1,0:T(2,128)(2,1)S(1)} %reshape_reshape_reshape.4), kind=kLoop, calls=%fused_computation.7 | loop fusion | flops 1568768 | bytes 1073152
  97.9 0.1 broadcast_multiply_fusion
  98.0 0.4 copy.49
  98.5 3.8 %fusion = (f32[128,16,2]{0,2,1:T(2,128)S(1)}, f32[16,512,128,2]{2,1,3,0:T(8,128)S(1)}) fusion(pred[128,512]{0,1:T(8,128)(4,1)S(1)} %compare_and_fusion, bf16[128,16,2,128]{3,2,1,0:T(2,128)(2,1)S(1)} %reshape_reshape_reshape.4, bf16[512,16,128,1]{2,1,0,3:T(8,128)(2,1)} %bitcast.96), kind=kOutput, calls=%fused_computation.3 | convolution fusion | flops 543158272 | bytes 11616256 | tf_op jit(solution)/shard_map/while/body/eval_jaxpr/rgjd,kgd->rgjk/dot_general | solution.py:95
  102.3 0.0 copy-start
  102.3 0.0 copy-start.2
  102.4 2.1 %convert_reduce_fusion = f32[128,16,2]{0,2,1:T(2,128)S(1)} fusion(f32[128,16,2]{0,2,1:T(2,128)S(1)} %get-tuple-element.31, f32[16,512,128,2]{2,1,3,0:T(8,128)S(1)} %get-tuple-element.34, pred[128,512]{0,1:T(8,128)(4,1)S(1)} %compare_and_fusion), kind=kLoop, calls=%fused_computation.1 | loop fusion | flops 14675968 | bytes 8486912 | tf_op jit(solution)/shard_map/while/body/eval_jaxpr/reduce_sum | solution.py:111
  104.4 1.4 copy-done
  105.8 0.1 copy.32
  105.9 0.1 copy.31
  106.0 0.0 copy-done.2
  106.1 6.9 %multiply_add_fusion = f32[16,128,2,128]{1,3,2,0:T(8,128)} fusion(bf16[512,16,128,1]{0,2,3,1:T(8,128)(2,1)S(1)} %bitcast.95, f32[16,128]{1,0:T(8,128)S(1)} %bitcast.108, f32[16,128,2]{1,2,0:T(2,128)S(1)} %bitcast.105, f32[16,512,128,2]{2,1,3,0:T(8,128)} %copy-done, f32[128,16,2]{0,2,1:T(2,128)S(1)} %get-tuple-element.31, ...), kind=kOutput, calls=%fused_computation.8 | convolution fusion | flops 548405248 | bytes 12689408 | tf_op jit(solution)/shard_map/while/body/eval_jaxpr/rgjk,kgd->rgjd/dot_general | solution.py:114
  113.0 4.9 %copy.30 = f32[1,128,4096]{2,0,1:T(1,128)S(1)} copy(f32[1,128,4096]{1,2,0:T(8,128)} %bitcast.97) | data formatting | bytes 4194304 | tf_op jit(solution)/shard_map/while/body/jit(dynamic_update_index_in_dim)/broadcast_in_dim | solution.py:127
  117.9 8.9 %concatenate.3 = f32[1,128,4160]{2,0,1:T(1,128)} concatenate(f32[1,128,4096]{2,0,1:T(1,128)S(1)} %copy.30, f32[1,128,32]{2,0,1:T(1,128)S(1)} %copy.31, f32[1,128,32]{2,0,1:T(1,128)S(1)} %copy.32), dimensions={2} | concatenate | bytes 4259840 | tf_op jit(solution)/shard_map/concatenate | solution.py:43
  126.8 14.4 %all-to-all-start = ((f32[1,128,4160]{2,0,1:T(1,128)}), f32[1,128,4160]{2,0,1:T(1,128)S(1)}, u32[]{:S(2)}, u32[]{:S(2)}) async-start(f32[1,128,4160]{2,0,1:T(1,128)} %concatenate.3), calls=%async_computation | async-start | bytes 4325376 | tf_op jit(solution)/shard_map/all_to_all | solution.py:45
  141.2 51.9 %all-to-all-done = f32[1,128,4160]{2,0,1:T(1,128)S(1)} async-done(((f32[1,128,4160]{2,0,1:T(1,128)}), f32[1,128,4160]{2,0,1:T(1,128)S(1)}, u32[]{:S(2)}, u32[]{:S(2)}) %all-to-all-start) | async-done | bytes 2129952 | tf_op jit(solution)/shard_map/all_to_all | solution.py:45
  193.1 0.2 slice_reduce_fusion
  193.2 0.2 fusion.5
  193.5 0.6 mul.50
  194.1 2.6 %fusion.3 = f32[4096]{0:T(1024)S(1)} fusion(f32[128,1,4096]{2,1,0:T(1,128)S(1)} %bitcast.91, f32[128,1,4160]{2,1,0:T(1,128)S(1)} %bitcast.90), kind=kLoop, calls=%fused_computation.9 | loop fusion | flops 1044480 | bytes 4210688 | tf_op jit(solution)/shard_map/reduce_sum | solution.py:136
  196.7 0.1 div.62
  196.8 0.6 fusion.6
  (12 shorter events, 0.1 us)
Async XLA Ops:
  6.5 52.3 %copy-start.1 = (bf16[512,2048]{1,0:T(8,128)(2,1)S(1)}, bf16[512,2048]{1,0:T(8,128)(2,1)}, u32[]{:S(2)}) copy-start(bf16[512,2048]{1,0:T(8,128)(2,1)} %param.10) | copy-start | bytes 6291460
  6.5 86.0 %all-gather.5.cloned.1.call-start = ((), (), s32[]{:S(2)}) async-start(), calls=%async_computation.1 | async-start | bytes 1572864 | tf_op jit(solution)/shard_map/all_gather | solution.py:31
  60.9 3.9 %copy-start.3 = (bf16[1,2048]{1,0:T(2,128)(2,1)S(1)}, bf16[1,2048]{1,0:T(2,128)(2,1)}, u32[]{:S(2)}) copy-start(bf16[1,2048]{1,0:T(2,128)(2,1)} %param.9) | copy-start | bytes 12292
  60.9 4.0 %copy-start.4 = (bf16[1,2048]{1,0:T(2,128)(2,1)S(1)}, bf16[1,2048]{1,0:T(2,128)(2,1)}, u32[]{:S(2)}) copy-start(bf16[1,2048]{1,0:T(2,128)(2,1)} %param.8) | copy-start | bytes 12292
  102.3 3.6 %copy-start = (f32[16,512,128,2]{2,1,3,0:T(8,128)}, f32[16,512,128,2]{2,1,3,0:T(8,128)S(1)}, u32[]{:S(2)}) copy-start(f32[16,512,128,2]{2,1,3,0:T(8,128)S(1)} %get-tuple-element.34) | copy-start | bytes 25165828
  102.3 3.7 %copy-start.2 = (bf16[512,2048]{0,1:T(8,128)(2,1)S(1)}, bf16[512,2048]{0,1:T(8,128)(2,1)}, u32[]{:S(2)}) copy-start(bf16[512,2048]{0,1:T(8,128)(2,1)} %copy.45) | copy-start | bytes 6291460
  126.8 66.3 %all-to-all-start = ((f32[1,128,4160]{2,0,1:T(1,128)}), f32[1,128,4160]{2,0,1:T(1,128)S(1)}, u32[]{:S(2)}, u32[]{:S(2)}) async-start(f32[1,128,4160]{2,0,1:T(1,128)} %concatenate.3), calls=%async_computation | async-start | bytes 4325376 | tf_op jit(solution)/shard_map/all_to_all | solution.py:45
Sparse Core Ops, SparseCore 0:
  57.7 34.7 all-gather.4
where the time goes:
time: 206 us; the launch traced here: 204 us
  waiting for transfers between devices  79.3 us (38%)
  blocking collectives  49.6 us (24%)
  local copies, waits for them, and re-layouts  26.9 us (13%)
  between operations  15 us (7%)
  starting transfers between devices  14.4 us (7%)
  matrix products  10.7 us (5%)
  other arithmetic  8.34 us (4%)
    all_to_all x1, waiting for transfers between devices, side_by_side(): lax.all_to_all(both, axis, split_axis=split_dim, concat_axis=concat_dim,...  51.9 us
    all_gather x1, blocking collectives, stacked_from(): tiles = lax.all_gather(tiles, axes[k])  49.6 us
    all_gather x1, waiting for transfers between devices, stacked_from(): tiles = lax.all_gather(tiles, axes[k])  27.4 us
    all_to_all x1, starting transfers between devices, side_by_side(): lax.all_to_all(both, axis, split_axis=split_dim, concat_axis=concat_dim,...  14.4 us
    concatenate x1, local copies, waits for them, and re-layouts, side_by_side(): both = jnp.concatenate(arrays, axis=along)  8.95 us
    dot_general x1, matrix products, one_block(): jnp.einsum('rgjk,kgd->rgjd', weights_doc, value_doc, preferred_element_ty...  6.95 us
    unnamed x13, local copies, waits for them, and re-layouts  5.2 us
    broadcast_in_dim x1, local copies, waits for them, and re-layouts, local(): numer, row_top, denom = lax.map(one_block, starts)  4.85 us
  transfers between devices with their start and end apart: 2, of which 2 were waited for; matrix products, arithmetic and copies ran while one was open for 3% of the time, Pallas kernels for 0%

commit v1 on v0

v1 whole, which is shorter than its diff:
```python
import functools
import math

import jax
import jax.numpy as jnp
from jax import lax
from jax.experimental import pallas as pl
from jax.experimental.pallas import tpu as pltpu
from jax.sharding import PartitionSpec as P

H = 32
KVH = 16
HD = 128
QSCALE = 144
NEG = -1e30
HALF = H // 2
KVHALF = KVH // 2
GROUP = H // KVH
SCALE = QSCALE ** (-0.5) * math.log2(math.e)
CHUNKS = 4
ROW_TILES = 24

f32 = jnp.float32
bf16 = jnp.bfloat16


def kernel(
    nb,
    q_hbm, kq_hbm, vq_hbm, k_hbm, v_hbm, len_hbm, off_hbm,
    out_ref,
    q_in, kq_in, vq_in, len_s, off_s, rows32, send_rows, got_q, got_kv, turn32,
    mine_q, all_q, keys, vals, parts, stats, own_o, own_l, got_o, got_l, row_o, last,
    loc, ex_send, ex_recv, s1_send, s1_recv, s2_send, s2_recv,
    r1_send, r1_recv, st_recv, r2_send, r2_recv,
):
    rb = 2 * nb
    rows = rb * nb
    groups = max(rb // 8, 1)
    gs = rb // groups
    doc = k_hbm.shape[0]
    width = KVHALF * HD
    me = lax.axis_index("seq")
    c = lax.rem(me, 2)
    chip = me // 2
    x = lax.rem(chip, nb)
    y = chip // nb
    a = x * (1 - c) + y * c
    b = y * (1 - c) + x * c

    def dev(xx, yy, cc):
        return (yy * nb + xx) * 2 + cc

    def role_dev(aa, bb, cc):
        return dev(aa * (1 - c) + bb * c, bb * (1 - c) + aa * c, cc)

    def step(v, t):
        return lax.rem(v + t, nb)

    order = sorted(range(1, nb), key=lambda t: -min(t, nb - t))

    def send(src, dst, ssem, rsem, target):
        pltpu.make_async_remote_copy(
            src_ref=src, dst_ref=dst, send_sem=ssem, recv_sem=rsem,
            device_id={"seq": target}, device_id_type=pl.DeviceIdType.MESH,
        ).start()

    def await_bytes(ref, sem):
        pltpu.make_async_copy(ref, ref, sem).wait()

    mine = pl.ds(pl.multiple_of(c * width, 128), width)
    other = pl.ds(pl.multiple_of((1 - c) * width, 128), width)
    small = [
        pltpu.make_async_copy(q_hbm, q_in, loc.at[0]),
        pltpu.make_async_copy(kq_hbm, kq_in, loc.at[1]),
        pltpu.make_async_copy(vq_hbm, vq_in, loc.at[2]),
        pltpu.make_async_copy(len_hbm, len_s, loc.at[3]),
        pltpu.make_async_copy(off_hbm, off_s, loc.at[4]),
    ]
    large = [
        pltpu.make_async_copy(k_hbm.at[:, mine], keys.at[c], loc.at[5]),
        pltpu.make_async_copy(v_hbm.at[:, mine], vals.at[c], loc.at[6]),
    ]
    barrier = pltpu.get_barrier_semaphore()
    for t in range(1, nb):
        for cc in range(2):
            for target in (dev(step(x, t), y, cc), dev(x, step(y, t), cc)):
                pl.semaphore_signal(
                    barrier, inc=1, device_id={"seq": target},
                    device_id_type=pl.DeviceIdType.MESH,
                )
    pl.semaphore_signal(
        barrier, inc=1, device_id={"seq": dev(x, y, 1 - c)},
        device_id_type=pl.DeviceIdType.MESH,
    )
    for copy in small + large:
        copy.start()
    for copy in small:
        copy.wait()
    for h in range(H):
        rows32[h : h + 1, :] = q_in[:, h * HD : (h + 1) * HD].astype(f32)
    for g in range(KVH):
        rows32[H + g : H + g + 1, :] = kq_in[:, g * HD : (g + 1) * HD].astype(f32)
        rows32[H + KVH + g : H + KVH + g + 1, :] = vq_in[:, g * HD : (g + 1) * HD].astype(f32)
    for r in range(2):
        send_rows[r, 0] = rows32[r * HALF : (r + 1) * HALF, :].astype(bf16)
        at = H + r * KVHALF
        send_rows[r, 1] = jnp.concatenate(
            [rows32[at : at + KVHALF, :], rows32[at + KVH : at + KVH + KVHALF, :]], axis=0
        ).astype(bf16)
    got_q[b * 2 + c] = send_rows[c, 0]
    got_kv[a * 2 + c] = send_rows[c, 1]
    pl.semaphore_wait(barrier, 4 * (nb - 1) + 1)

    for t in order:
        send(send_rows.at[0, 0], got_q.at[y * 2 + c], s1_send, s1_recv.at[0], dev(x, step(y, t), 0))
        send(send_rows.at[1, 0], got_q.at[x * 2 + c], s1_send, s1_recv.at[0], dev(step(x, t), y, 1))
    send(send_rows.at[1 - c, 0], got_q.at[a * 2 + c], s1_send, s1_recv.at[0], dev(x, y, 1 - c))
    for t in order:
        send(send_rows.at[0, 1], got_kv.at[x * 2 + c], s1_send, s1_recv.at[1], dev(step(x, t), y, 0))
        send(send_rows.at[1, 1], got_kv.at[y * 2 + c], s1_send, s1_recv.at[1], dev(x, step(y, t), 1))
    send(send_rows.at[1 - c, 1], got_kv.at[b * 2 + c], s1_send, s1_recv.at[1], dev(x, y, 1 - c))
    send(k_hbm.at[:, other], keys.at[c], ex_send.at[0], ex_recv.at[0], dev(x, y, 1 - c))
    send(v_hbm.at[:, other], vals.at[c], ex_send.at[1], ex_recv.at[1], dev(x, y, 1 - c))

    await_bytes(got_q.at[0 : rb - 1], s1_recv.at[0])
    for i in range(rb):
        turn32[i * HALF : (i + 1) * HALF, :] = got_q[i].astype(f32)
    for h in range(HALF):
        block = turn32[pl.ds(h, rb, stride=HALF), :].astype(bf16)
        mine_q[h] = block
        all_q[h, pl.ds(pl.multiple_of(a * rb, rb), rb), :] = block

    per = HALF // CHUNKS
    for j in range(CHUNKS):
        for t in order:
            send(
                mine_q.at[pl.ds(j * per, per)],
                all_q.at[pl.ds(j * per, per), pl.ds(pl.multiple_of(a * rb, rb), rb), :],
                s2_send, s2_recv.at[j], role_dev(step(a, t), b, c),
            )

    await_bytes(got_kv.at[0 : rb - 1], s1_recv.at[1])
    for i in range(rb):
        turn32[i * HALF : (i + 1) * HALF, :] = got_kv[i].astype(f32)

    def row_of(aa, bb, cc):
        return dev(aa * (1 - c) + bb * c, bb * (1 - c) + aa * c, cc)

    spot = lax.rem(lax.broadcasted_iota(jnp.int32, (GROUP * rb, rb), 0), rb)
    key_spot = lax.broadcasted_iota(jnp.int32, (GROUP * rb, rb), 1)
    see = row_of(key_spot // 2, b, lax.rem(key_spot, 2)) <= row_of(a, spot // 2, lax.rem(spot, 2))
    lane = lax.broadcasted_iota(jnp.int32, (gs, 128), 1)
    own = jnp.full((gs, 128), NEG, f32)
    for g in range(KVHALF):
        key = turn32[pl.ds(g, rb, stride=HALF), :].astype(bf16)
        val = turn32[pl.ds(KVHALF + g, rb, stride=HALF), :].astype(bf16)
        q = mine_q[g * GROUP : (g + 1) * GROUP].reshape(GROUP * rb, HD)
        s = lax.dot_general(q, key, (((1,), (1,)), ((), ())), preferred_element_type=f32)
        s = jnp.where(see, s, NEG)
        top = jnp.max(s, axis=1, keepdims=True)
        p = jnp.exp2((s - top) * SCALE).astype(bf16)
        den = jnp.sum(p.astype(f32), axis=1, keepdims=True)
        num = jnp.dot(p, val, preferred_element_type=f32)
        own_o[g * GROUP : (g + 1) * GROUP] = (num / den).reshape(GROUP, rb, HD)
        level = top * SCALE + jnp.log2(den)
        for i in range(GROUP):
            for k in range(groups):
                at = i * rb + k * gs
                own = jnp.where(lane == k * HALF + g * GROUP + i, level[at : at + gs], own)
    own_l[...] = own

    for i in range(nb):
        stats[i] = jnp.full((gs, 128), NEG, f32)
    for copy in large:
        copy.wait()
    await_bytes(keys.at[1 - c], ex_recv.at[0])
    await_bytes(vals.at[1 - c], ex_recv.at[1])
    offset = off_s[0]
    places = lax.broadcasted_iota(jnp.int32, (1, doc), 1)
    seen = [places + (chip * 2 + blk) * doc < offset for blk in range(2)]
    ones = jnp.ones((doc, HD), bf16)

    def chunk(j, carry):
        first = j * per
        await_bytes(
            all_q.at[pl.ds(first, per), 0 : (nb - 1) * rb, :], s2_recv.at[j]
        )
        for u in range(per // GROUP):
            head = first + u * GROUP
            col = pl.ds(pl.multiple_of((head // GROUP) * HD, 128), HD)
            q = all_q[pl.ds(head, GROUP)].reshape(GROUP * rows, HD)
            tops, nums, dens = [], [], []
            for blk in range(2):
                s = lax.dot_general(
                    q, keys[blk, :, col], (((1,), (1,)), ((), ())), preferred_element_type=f32
                )
                s = jnp.where(seen[blk], s, NEG)
                top = jnp.max(s, axis=1, keepdims=True)
                p = jnp.exp2((s - top) * SCALE).astype(bf16)
                both = jnp.dot(
                    p, jnp.concatenate([vals[blk, :, col], ones], axis=1),
                    preferred_element_type=f32,
                )
                tops.append(top)
                nums.append(both[:, :HD])
                dens.append(both[:, HD:])
            top = jnp.maximum(tops[0], tops[1])
            w = [jnp.exp2((m - top) * SCALE) for m in tops]
            den = dens[0] * w[0] + dens[1] * w[1]
            inv = 1.0 / den
            o = nums[0] * (w[0] * inv) + nums[1] * (w[1] * inv)
            level = top * SCALE + jnp.log2(den)
            parts[pl.ds(head, GROUP)] = o.reshape(GROUP, rows, HD).astype(bf16)
            for i in range(nb):
                tile = stats[i]
                for z in range(GROUP):
                    for k in range(groups):
                        at = z * rows + i * rb + k * gs
                        tile = jnp.where(lane == k * HALF + head + z, level[at : at + gs], tile)
                stats[i] = tile
        for t in order:
            peer = step(a, t)
            send(
                parts.at[pl.ds(first, per), pl.ds(pl.multiple_of(peer * rb, rb), rb), :],
                got_o.at[a, pl.ds(first, per)],
                r1_send, r1_recv.at[j], role_dev(peer, b, c),
            )
        return carry

    lax.fori_loop(0, CHUNKS, chunk, 0)
    for t in order:
        peer = step(a, t)
        send(stats.at[peer], got_l.at[a], r1_send, st_recv, role_dev(peer, b, c))

    await_bytes(got_l.at[0 : nb - 1], st_recv)
    levels = [stats[a]] + [got_l[step(a, t)] for t in range(1, nb)] + [own_l[...]]
    top = functools.reduce(jnp.maximum, levels)
    weights = [jnp.exp2(v - top) for v in levels]
    total = functools.reduce(jnp.add, weights)
    inv = 1.0 / total
    weights = [w * inv for w in weights]
    level = top + jnp.log2(total)
    for j in range(CHUNKS):
        await_bytes(got_o.at[0 : nb - 1, pl.ds(j * per, per)], r1_recv.at[j])
        for h in range(j * per, (j + 1) * per):
            full = [parts[h, pl.ds(pl.multiple_of(a * rb, rb), rb), :].astype(f32)]
            full += [got_o[step(a, t), h].astype(f32) for t in range(1, nb)]
            full += [own_o[h]]
            for k in range(groups):
                at = k * HALF + h
                acc = weights[0][:, at : at + 1] * full[0][k * gs : (k + 1) * gs]
                for w, part in zip(weights[1:], full[1:]):
                    acc += w[:, at : at + 1] * part[k * gs : (k + 1) * gs]
                row_o[pl.ds(k * gs * ROW_TILES + h, gs, stride=ROW_TILES), :] = acc
    for h in range(HALF // 2):
        for k in range(groups):
            at = k * HALF + h
            pair = jnp.where(
                lane < 64, level[:, at : at + 1], level[:, at + HALF // 2 : at + HALF // 2 + 1]
            )
            row_o[pl.ds(k * gs * ROW_TILES + HALF + h, gs, stride=ROW_TILES), :] = pair

    def row_at(i):
        return pl.ds(pl.multiple_of(i * ROW_TILES, 8), ROW_TILES)

    for t in order:
        peer = step(b, t)
        for cc in range(2):
            send(
                row_o.at[row_at(peer * 2 + cc)], last.at[c * nb + b],
                r2_send, r2_recv, role_dev(a, peer, cc),
            )
    send(
        row_o.at[row_at(b * 2 + 1 - c)], last.at[c * nb + b],
        r2_send, r2_recv, dev(x, y, 1 - c),
    )
    last[c * nb + b] = row_o[row_at(b * 2 + c), :]
    await_bytes(last.at[0 : 2 * nb - 1], r2_recv)

    live = jnp.full((HALF // 2, 128), me, jnp.int32) < len_s[0]
    for r in range(2):
        levels = [last[r * nb + i, HALF:, :] for i in range(nb)]
        top = functools.reduce(jnp.maximum, levels)
        weights = [jnp.exp2(v - top) for v in levels]
        inv = 1.0 / functools.reduce(jnp.add, weights)
        outs = []
        for k in range(2):
            acc = None
            for i in range(nb):
                w = weights[i] * inv
                term = w[:, k * 64 : k * 64 + 1] * last[
                    r * nb + i, k * HALF // 2 : (k + 1) * HALF // 2, :
                ]
                acc = term if acc is None else acc + term
            outs.append(jnp.where(live, acc, 0.0))
        out_ref[r * HALF : (r + 1) * HALF, :] = jnp.concatenate(outs, axis=0).astype(bf16)

    await_bytes(got_q.at[0 : rb - 1], s1_send)
    await_bytes(got_kv.at[0 : rb - 1], s1_send)
    for i, buf in enumerate((keys, vals)):
        await_bytes(buf.at[c], ex_send.at[i])
    await_bytes(all_q.at[:, 0 : (nb - 1) * rb, :], s2_send)
    await_bytes(got_o.at[0 : nb - 1], r1_send)
    await_bytes(got_l.at[0 : nb - 1], r1_send)
    await_bytes(last.at[0 : 2 * nb - 1], r2_send)


def local(nb, q, kq, vq, k, v, lengths, offsets):
    rb = 2 * nb
    rows = rb * nb
    doc = k.shape[0]
    gs = rb // max(rb // 8, 1)
    dma = pltpu.SemaphoreType.DMA
    out = pl.pallas_call(
        functools.partial(kernel, nb),
        out_shape=jax.ShapeDtypeStruct((H, HD), bf16),
        in_specs=[pl.BlockSpec(memory_space=pl.ANY)] * 7,
        out_specs=pl.BlockSpec(memory_space=pltpu.VMEM),
        scratch_shapes=[
            pltpu.VMEM((1, H * HD), bf16),
            pltpu.VMEM((1, KVH * HD), bf16),
            pltpu.VMEM((1, KVH * HD), bf16),
            pltpu.SMEM((1,), jnp.int32),
            pltpu.SMEM((1,), jnp.int32),
            pltpu.VMEM((H + 2 * KVH, HD), f32),
            pltpu.VMEM((2, 2, HALF, HD), bf16),
            pltpu.VMEM((rb, HALF, HD), bf16),
            pltpu.VMEM((rb, HALF, HD), bf16),
            pltpu.VMEM((rb * HALF, HD), f32),
            pltpu.VMEM((HALF, rb, HD), bf16),
            pltpu.VMEM((HALF, rows, HD), bf16),
            pltpu.VMEM((2, doc, KVHALF * HD), bf16),
            pltpu.VMEM((2, doc, KVHALF * HD), bf16),
            pltpu.VMEM((HALF, rows, HD), bf16),
            pltpu.VMEM((nb, gs, 128), f32),
            pltpu.VMEM((HALF, rb, HD), f32),
            pltpu.VMEM((gs, 128), f32),
            pltpu.VMEM((nb, HALF, rb, HD), bf16),
            pltpu.VMEM((nb, gs, 128), f32),
            pltpu.VMEM((rb * ROW_TILES, HD), f32),
            pltpu.VMEM((2 * nb, ROW_TILES, HD), f32),
            dma((7,)), dma((2,)), dma((2,)), dma, dma((2,)), dma, dma((CHUNKS,)),
            dma, dma((CHUNKS,)), dma, dma, dma,
        ],
        compiler_params=pltpu.CompilerParams(
            collective_id=0, has_side_effects=True, vmem_limit_bytes=56 * 1024 * 1024
        ),
    )(q, kq, vq, k, v, lengths, offsets)
    return out.reshape(1, H * HD)


def solution(mesh):
    nb = math.isqrt(mesh.shape["seq"] // 2)
    rows = P(("grp", "seq"), None)
    return jax.shard_map(
        functools.partial(local, nb),
        mesh=mesh,
        in_specs=(rows, rows, rows, rows, rows, P("grp"), P("grp")),
        out_specs=rows,
        check_vma=False,
    )
```

time: 206 us -> 53.3 us (0.26)
  waiting for transfers between devices: 79.3 us -> 0 us
  Pallas kernels: 0 us -> 50.4 us
  blocking collectives: 49.6 us -> 0 us
  local copies, waits for them, and re-layouts: 26.9 us -> 1.32 us
  starting transfers between devices: 14.4 us -> 0 us
  between operations: 15 us -> 1.3 us
  matrix products: 10.7 us -> 0 us
  other arithmetic: 8.34 us -> 0 us
    all_to_all x1 -> x0, waiting for transfers between devices: 51.9 us -> none  [side_by_side(): lax.all_to_all(both, axis, split_axis=split_dim, concat_axis=concat_dim,...]
    pallas_call x0 -> x1, Pallas kernels: none -> 50.4 us  [local(): pl.pallas_call(functools.partial(kernel, nb), out_shape=jax.ShapeDtypeStr...]
    all_gather x1 -> x0, blocking collectives: 49.6 us -> none  [stacked_from(): tiles = lax.all_gather(tiles, axes[k])]
    all_gather x1 -> x0, waiting for transfers between devices: 27.4 us -> none  [stacked_from(): tiles = lax.all_gather(tiles, axes[k])]
    all_to_all x1 -> x0, starting transfers between devices: 14.4 us -> none  [side_by_side(): lax.all_to_all(both, axis, split_axis=split_dim, concat_axis=concat_dim,...]
    dot_general x2 -> x0, matrix products: 10.7 us -> none  [the longest x1 6.95 us: one_block(): jnp.einsum('rgjk,kgd->rgjd', weights_doc, value_doc, preferred_element_ty...]
    concatenate x1 -> x0, local copies, waits for them, and re-layouts: 8.95 us -> none  [side_by_side(): both = jnp.concatenate(arrays, axis=along)]
    reduce_sum x3 -> x0, other arithmetic: 4.93 us -> none  [the longest x1 2.63 us: local(): jnp.sum(got_num.reshape(device_count, rows_local, H, HD) * rescale[:, :,...]
  transfers between devices with their start and end apart: 2 -> 0, of which waited for: 2 -> 0; matrix products, arithmetic and copies ran while one was open for 3% -> 0% of each run, Pallas kernels for 0% -> 0%
where the time goes in v1:
time: 53.3 us; the launch traced here: 53 us
  Pallas kernels  50.4 us (95%)
  local copies, waits for them, and re-layouts  1.32 us (2%)
  between operations  1.3 us (2%)
    pallas_call x1, Pallas kernels, local(): pl.pallas_call(functools.partial(kernel, nb), out_shape=jax.ShapeDtypeStr...  50.4 us
    unnamed x1, local copies, waits for them, and re-layouts  1.32 us

profile of v1, /device:TPU:513, one launch (start us, length us, event | category | flops | bytes accessed | tf_op | source)
XLA Modules:
  0.0 53.0 jit_solution(10483804478347025778)
XLA Ops:
  1.3 50.4 %shard_map.73 = bf16[32,128]{1,0:T(8,128)(2,1)} custom-call(bf16[1,4096]{1,0:T(2,128)(2,1)} %q_hbm.1, bf16[1,2048]{1,0:T(2,128)(2,1)} %kq_hbm.1, bf16[1,2048]{1,0:T(2,128)(2,1)} %vq_hbm.1, bf16[512,2048]{1,0:T(8,128)(2,1)} %k_hbm.1, bf16[512,2048]{1,0:T(8,128)(2,1)} %v_hbm.1, s32[1]{0:T(128)S(6)} %copy.11.len_hbm, s32[1]{0:T(128)S(6)} %copy.12.off_hbm), custom_call_target="tpu_custom_call" | custom-call | tf_op jit(solution)/shard_map/pallas_call | solution.py:314
  51.7 1.3 %copy.10 = bf16[1,1,32,128]{3,1,2,0:T(2,128)(2,1)} copy(bf16[1,1,32,128]{3,2,1,0:T(8,128)(2,1)} %bitcast.5) | data formatting | bytes 16384

commit v2 on v1

--- a/solution.py
+++ b/solution.py
@@ -30,8 +30,10 @@
     out_ref,
     q_in, kq_in, vq_in, len_s, off_s, rows32, send_rows, got_q, got_kv, turn32,
     mine_q, all_q, keys, vals, parts, stats, own_o, own_l, got_o, got_l, row_o, last,
+    spare_q, first_q, first_o, first_l, pair_k, pair_v,
     loc, ex_send, ex_recv, s1_send, s1_recv, s2_send, s2_recv,
     r1_send, r1_recv, st_recv, r2_send, r2_recv,
+    here, spare_recv, relay_recv, relay_send, first_send, first_recv, back_send, back_recv,
 ):
     rb = 2 * nb
     rows = rb * nb
@@ -56,6 +58,9 @@
     def step(v, t):
         return lax.rem(v + t, nb)
 
+    zero = me == 0
+    rest = me > 0
+    stand = dev(0, 1, 0)
     order = sorted(range(1, nb), key=lambda t: -min(t, nb - t))
 
     def send(src, dst, ssem, rsem, target):
@@ -80,20 +85,33 @@
         pltpu.make_async_copy(k_hbm.at[:, mine], keys.at[c], loc.at[5]),
         pltpu.make_async_copy(v_hbm.at[:, mine], vals.at[c], loc.at[6]),
     ]
-    barrier = pltpu.get_barrier_semaphore()
-    for t in range(1, nb):
-        for cc in range(2):
-            for target in (dev(step(x, t), y, cc), dev(x, step(y, t), cc)):
-                pl.semaphore_signal(
-                    barrier, inc=1, device_id={"seq": target},
-                    device_id_type=pl.DeviceIdType.MESH,
-                )
-    pl.semaphore_signal(
-        barrier, inc=1, device_id={"seq": dev(x, y, 1 - c)},
-        device_id_type=pl.DeviceIdType.MESH,
-    )
     for copy in small + large:
         copy.start()
+    mate = dev(x, y, 1 - c)
+
+    def send_keys():
+        send(k_hbm.at[:, other], keys.at[c], ex_send.at[0], ex_recv.at[0], mate)
+        send(v_hbm.at[:, other], vals.at[c], ex_send.at[1], ex_recv.at[1], mate)
+
+    barrier = pltpu.get_barrier_semaphore()
+
+    def signal(sem, target):
+        pl.semaphore_signal(
+            sem, inc=1, device_id={"seq": target}, device_id_type=pl.DeviceIdType.MESH
+        )
+
+    @pl.when(rest)
+    def _():
+        for t in order:
+            for cc in range(2):
+                signal(barrier, dev(step(x, t), y, cc))
+                signal(barrier, dev(x, step(y, t), cc))
+        signal(barrier, dev(x, y, 1 - c))
+
+    @pl.when((x > 0) & (y > 0))
+    def _():
+        signal(barrier, 0)
+
     for copy in small:
         copy.wait()
     for h in range(H):
@@ -107,68 +125,149 @@
         send_rows[r, 1] = jnp.concatenate(
             [rows32[at : at + KVHALF, :], rows32[at + KVH : at + KVH + KVHALF, :]], axis=0
         ).astype(bf16)
-    got_q[b * 2 + c] = send_rows[c, 0]
     got_kv[a * 2 + c] = send_rows[c, 1]
-    pl.semaphore_wait(barrier, 4 * (nb - 1) + 1)
+
+    @pl.when(rest)
+    def _():
+        got_q[b * 2 + c] = send_rows[c, 0]
+
+    @pl.when(a == 0)
+    def _():
+        got_q[0] = jnp.zeros((HALF, HD), bf16)
+
+    line = 4 * (nb - 1) + 1
+    near = jnp.where((x == 0) | (y == 0), 1, 0)
+    pl.semaphore_wait(barrier, jnp.where(zero, 2 * nb * nb - 1, line - near))
+
+    @pl.when(zero)
+    def _():
+        signal(here, 1)
+        for t in order:
+            for cc in range(2):
+                signal(here, dev(t, 0, cc))
+        send_keys()
+        first_q[...] = send_rows[0, 0]
+        far = sorted(
+            ((xx, yy) for xx in range(nb) for yy in range(nb)),
+            key=lambda p: -min(p[0], nb - p[0]) - min(p[1], nb - p[1]),
+        )
+        for xx, yy in far:
+            for cc in range(2):
+                if xx or yy or cc:
+                    send(send_rows.at[cc, 0], first_q, first_send, first_recv, dev(xx, yy, cc))
+
+    my_block = pl.ds(pl.multiple_of(a * rb, rb), rb)
+    per = HALF // CHUNKS
+
+    def send_mate_row(k, slot):
+        send(send_rows.at[1 - c, k], slot, s1_send.at[k], s1_recv.at[k], mate)
+
+    @pl.when(rest)
+    def _():
+        for t in order:
+            to_0 = dev(x, step(y, t), 0)
+
+            @pl.when(to_0 > 0)
+            def _(to_0=to_0):
+                send(send_rows.at[0, 0], got_q.at[y * 2 + c], s1_send.at[0], s1_recv.at[0], to_0)
+
+            send(
+                send_rows.at[1, 0], got_q.at[x * 2 + c], s1_send.at[0], s1_recv.at[0],
+                dev(step(x, t), y, 1),
+            )
+
+        @pl.when(me > 1)
+        def _():
+            send_mate_row(0, got_q.at[a * 2 + c])
+
+    def send_row_0(target):
+        send(send_rows.at[0, 1], got_kv.at[x * 2 + c], s1_send.at[1], s1_recv.at[1], target)
 
     for t in order:
-        send(send_rows.at[0, 0], got_q.at[y * 2 + c], s1_send, s1_recv.at[0], dev(x, step(y, t), 0))
-        send(send_rows.at[1, 0], got_q.at[x * 2 + c], s1_send, s1_recv.at[0], dev(step(x, t), y, 1))
-    send(send_rows.at[1 - c, 0], got_q.at[a * 2 + c], s1_send, s1_recv.at[0], dev(x, y, 1 - c))
-    for t in order:
-        send(send_rows.at[0, 1], got_kv.at[x * 2 + c], s1_send, s1_recv.at[1], dev(step(x, t), y, 0))
-        send(send_rows.at[1, 1], got_kv.at[y * 2 + c], s1_send, s1_recv.at[1], dev(x, step(y, t), 1))
-    send(send_rows.at[1 - c, 1], got_kv.at[b * 2 + c], s1_send, s1_recv.at[1], dev(x, y, 1 - c))
-    send(k_hbm.at[:, other], keys.at[c], ex_send.at[0], ex_recv.at[0], dev(x, y, 1 - c))
-    send(v_hbm.at[:, other], vals.at[c], ex_send.at[1], ex_recv.at[1], dev(x, y, 1 - c))
-
-    await_bytes(got_q.at[0 : rb - 1], s1_recv.at[0])
-    for i in range(rb):
-        turn32[i * HALF : (i + 1) * HALF, :] = got_q[i].astype(f32)
-    for h in range(HALF):
-        block = turn32[pl.ds(h, rb, stride=HALF), :].astype(bf16)
-        mine_q[h] = block
-        all_q[h, pl.ds(pl.multiple_of(a * rb, rb), rb), :] = block
-
-    per = HALF // CHUNKS
-    for j in range(CHUNKS):
-        for t in order:
-            send(
-                mine_q.at[pl.ds(j * per, per)],
-                all_q.at[pl.ds(j * per, per), pl.ds(pl.multiple_of(a * rb, rb), rb), :],
-                s2_send, s2_recv.at[j], role_dev(step(a, t), b, c),
-            )
-
-    await_bytes(got_kv.at[0 : rb - 1], s1_recv.at[1])
-    for i in range(rb):
-        turn32[i * HALF : (i + 1) * HALF, :] = got_kv[i].astype(f32)
-
-    def row_of(aa, bb, cc):
-        return dev(aa * (1 - c) + bb * c, bb * (1 - c) + aa * c, cc)
-
-    spot = lax.rem(lax.broadcasted_iota(jnp.int32, (GROUP * rb, rb), 0), rb)
-    key_spot = lax.broadcasted_iota(jnp.int32, (GROUP * rb, rb), 1)
-    see = row_of(key_spot // 2, b, lax.rem(key_spot, 2)) <= row_of(a, spot // 2, lax.rem(spot, 2))
+        to_0 = dev(step(x, t), y, 0)
+
+        @pl.when(to_0 > 0)
+        def _(to_0=to_0):
+            send_row_0(to_0)
+
+        send(
+            send_rows.at[1, 1], got_kv.at[y * 2 + c], s1_send.at[1], s1_recv.at[1],
+            dev(x, step(y, t), 1),
+        )
+
+    @pl.when(me != 1)
+    def _():
+        send_mate_row(1, got_kv.at[b * 2 + c])
+
+    @pl.when(me > 1)
+    def _():
+        send_keys()
+
+    @pl.when(rest)
+    def _():
+        @pl.when(a == 0)
+        def _():
+            await_bytes(got_q.at[0 : rb - 2], s1_recv.at[0])
+
+        @pl.when(a > 0)
+        def _():
+            await_bytes(got_q.at[0 : rb - 1], s1_recv.at[0])
+
+        for i in range(rb):
+            turn32[i * HALF : (i + 1) * HALF, :] = got_q[i].astype(f32)
+        for h in range(HALF):
+            block = turn32[pl.ds(h, rb, stride=HALF), :].astype(bf16)
+            mine_q[h] = block
+            all_q[h, my_block, :] = block
+        for j in range(CHUNKS):
+            some = pl.ds(j * per, per)
+
+            @pl.when(me == stand)
+            def _(some=some, j=j):
+                send(
+                    mine_q.at[some], spare_q.at[some, my_block, :],
+                    relay_send.at[0], relay_recv.at[j], 1,
+                )
+
+            for t in order:
+                target = role_dev(step(a, t), b, c)
+
+                @pl.when(target > 0)
+                def _(some=some, target=target, j=j):
+                    send(
+                        mine_q.at[some], all_q.at[some, my_block, :],
+                        s2_send, s2_recv.at[j], target,
+                    )
+
+                @pl.when(target == 0)
+                def _(some=some, j=j):
+                    send(
+                        mine_q.at[some], spare_q.at[some, my_block, :],
+                        s2_send, spare_recv.at[j], 1,
+                    )
+
+    @pl.when((y == 0) & rest)
+    def _():
+        pl.semaphore_wait(here, 1)
+
+        @pl.when(me == 1)
+        def _():
+            send_keys()
+            send_mate_row(1, got_kv.at[b * 2 + c])
+            for j in range(CHUNKS):
+                block = spare_q.at[pl.ds(j * per, per), 0:rb, :]
+                await_bytes(block, relay_recv.at[j])
+                for t in order:
+                    send(
+                        block, all_q.at[pl.ds(j * per, per), 0:rb, :],
+                        relay_send.at[1], s2_recv.at[j], dev(t, 0, 0),
+                    )
+
+        @pl.when(me > 1)
+        def _():
+            send_row_0(0)
+
     lane = lax.broadcasted_iota(jnp.int32, (gs, 128), 1)
-    own = jnp.full((gs, 128), NEG, f32)
-    for g in range(KVHALF):
-        key = turn32[pl.ds(g, rb, stride=HALF), :].astype(bf16)
-        val = turn32[pl.ds(KVHALF + g, rb, stride=HALF), :].astype(bf16)
-        q = mine_q[g * GROUP : (g + 1) * GROUP].reshape(GROUP * rb, HD)
-        s = lax.dot_general(q, key, (((1,), (1,)), ((), ())), preferred_element_type=f32)
-        s = jnp.where(see, s, NEG)
-        top = jnp.max(s, axis=1, keepdims=True)
-        p = jnp.exp2((s - top) * SCALE).astype(bf16)
-        den = jnp.sum(p.astype(f32), axis=1, keepdims=True)
-        num = jnp.dot(p, val, preferred_element_type=f32)
-        own_o[g * GROUP : (g + 1) * GROUP] = (num / den).reshape(GROUP, rb, HD)
-        level = top * SCALE + jnp.log2(den)
-        for i in range(GROUP):
-            for k in range(groups):
-                at = i * rb + k * gs
-                own = jnp.where(lane == k * HALF + g * GROUP + i, level[at : at + gs], own)
-    own_l[...] = own
-
     for i in range(nb):
         stats[i] = jnp.full((gs, 128), NEG, f32)
     for copy in large:
@@ -182,9 +281,21 @@
 
     def chunk(j, carry):
         first = j * per
-        await_bytes(
-            all_q.at[pl.ds(first, per), 0 : (nb - 1) * rb, :], s2_recv.at[j]
-        )
+
+        @pl.when(me == 1)
+        def _():
+            some = pl.ds(first, per)
+            await_bytes(spare_q.at[some, rb:, :], spare_recv.at[j])
+            send(spare_q.at[some], all_q.at[some], relay_send.at[2], s2_recv.at[j], 0)
+
+        @pl.when(zero)
+        def _():
+            await_bytes(all_q.at[pl.ds(first, per)], s2_recv.at[j])
+
+        @pl.when(rest)
+        def _():
+            await_bytes(all_q.at[pl.ds(first, per), 0 : (nb - 1) * rb, :], s2_recv.at[j])
+
         for u in range(per // GROUP):
             head = first + u * GROUP
             col = pl.ds(pl.multiple_of((head // GROUP) * HD, 128), HD)
@@ -223,14 +334,84 @@
             send(
                 parts.at[pl.ds(first, per), pl.ds(pl.multiple_of(peer * rb, rb), rb), :],
                 got_o.at[a, pl.ds(first, per)],
-                r1_send, r1_recv.at[j], role_dev(peer, b, c),
+                r1_send.at[0], r1_recv.at[j], role_dev(peer, b, c),
             )
         return carry
 
     lax.fori_loop(0, CHUNKS, chunk, 0)
     for t in order:
         peer = step(a, t)
-        send(stats.at[peer], got_l.at[a], r1_send, st_recv, role_dev(peer, b, c))
+        send(stats.at[peer], got_l.at[a], r1_send.at[1], st_recv, role_dev(peer, b, c))
+
+    await_bytes(got_kv.at[0 : rb - 1], s1_recv.at[1])
+    for i in range(rb):
+        turn32[i * HALF : (i + 1) * HALF, :] = got_kv[i].astype(f32)
+
+    def row_of(aa, bb, cc):
+        return dev(aa * (1 - c) + bb * c, bb * (1 - c) + aa * c, cc)
+
+    spot = lax.rem(lax.broadcasted_iota(jnp.int32, (GROUP * rb, rb), 0), rb)
+    key_spot = lax.broadcasted_iota(jnp.int32, (GROUP * rb, rb), 1)
+    see = row_of(key_spot // 2, b, lax.rem(key_spot, 2)) <= row_of(a, spot // 2, lax.rem(spot, 2))
+    own = jnp.full((gs, 128), NEG, f32)
+    for g in range(KVHALF):
+        key = turn32[pl.ds(g, rb, stride=HALF), :].astype(bf16)
+        val = turn32[pl.ds(KVHALF + g, rb, stride=HALF), :].astype(bf16)
+        q = all_q[g * GROUP : (g + 1) * GROUP, my_block, :].reshape(GROUP * rb, HD)
+        s = lax.dot_general(q, key, (((1,), (1,)), ((), ())), preferred_element_type=f32)
+        s = jnp.where(see, s, NEG)
+        top = jnp.max(s, axis=1, keepdims=True)
+        p = jnp.exp2((s - top) * SCALE).astype(bf16)
+        den = jnp.sum(p.astype(f32), axis=1, keepdims=True)
+        num = jnp.dot(p, val, preferred_element_type=f32)
+        own_o[g * GROUP : (g + 1) * GROUP] = (num / den).reshape(GROUP, rb, HD)
+        level = top * SCALE + jnp.log2(den)
+        for i in range(GROUP):
+            for k in range(groups):
+                at = i * rb + k * gs
+                own = jnp.where(lane == k * HALF + g * GROUP + i, level[at : at + gs], own)
+    own_l[...] = own
+
+    @pl.when(rest)
+    def _():
+        await_bytes(first_q, first_recv)
+
+    head_of = lax.broadcasted_iota(jnp.int32, (HALF, HD), 0) // GROUP
+    wide = jnp.concatenate(
+        [jnp.where(head_of == g, first_q[...], jnp.zeros((), bf16)) for g in range(KVHALF)], axis=1
+    )
+    tops, nums, dens = [], [], []
+    for blk in range(2):
+        s = lax.dot_general(
+            wide, keys[blk], (((1,), (1,)), ((), ())), preferred_element_type=f32
+        )
+        s = jnp.where(seen[blk], s, NEG)
+        top = jnp.max(s, axis=1, keepdims=True)
+        p = jnp.exp2((s - top) * SCALE).astype(bf16)
+        dens.append(jnp.sum(p.astype(f32), axis=1, keepdims=True))
+        num = jnp.dot(p, vals[blk], preferred_element_type=f32)
+        pick = jnp.zeros((HALF, HD), f32)
+        for g in range(KVHALF):
+            pick = jnp.where(head_of == g, num[:, g * HD : (g + 1) * HD], pick)
+        tops.append(top)
+        nums.append(pick)
+    top = jnp.maximum(tops[0], tops[1])
+    w = [jnp.exp2((m - top) * SCALE) for m in tops]
+    den = dens[0] * w[0] + dens[1] * w[1]
+    level = top * SCALE + jnp.log2(den)
+    half_lane = lax.broadcasted_iota(jnp.int32, (HALF // 2, 128), 1) < 64
+
+    def paired(v):
+        return jnp.where(half_lane, v[: HALF // 2], v[HALF // 2 :])
+
+    first_o[a] = ((nums[0] * w[0] + nums[1] * w[1]) / den).astype(bf16)
+    first_l[a] = paired(level)
+
+    @pl.when(a > 0)
+    def _():
+        target = role_dev(0, b, c)
+        send(first_o.at[a], first_o.at[a], back_send.at[0], back_recv.at[0], target)
+        send(first_l.at[a], first_l.at[a], back_send.at[1], back_recv.at[1], target)
 
     await_bytes(got_l.at[0 : nb - 1], st_recv)
     levels = [stats[a]] + [got_l[step(a, t)] for t in range(1, nb)] + [own_l[...]]
@@ -263,6 +444,40 @@
     def row_at(i):
         return pl.ds(pl.multiple_of(i * ROW_TILES, 8), ROW_TILES)
 
+    def spread(w, k):
+        return w[:, k * 64 : k * 64 + 1]
+
+    def merged(levels, values):
+        top = functools.reduce(jnp.maximum, levels)
+        weights = [jnp.exp2(v - top) for v in levels]
+        total = functools.reduce(jnp.add, weights)
+        inv = 1.0 / total
+        outs = []
+        for k in range(2):
+            terms = [
+                spread(w * inv, k) * v[k * HALF // 2 : (k + 1) * HALF // 2]
+                for w, v in zip(weights, values)
+            ]
+            outs.append(functools.reduce(jnp.add, terms))
+        return jnp.concatenate(outs, axis=0), top + jnp.log2(total)
+
+    @pl.when(a == 0)
+    def _():
+        await_bytes(first_o.at[0 : nb - 1], back_recv.at[0])
+        await_bytes(first_l.at[0 : nb - 1], back_recv.at[1])
+        pair = got_kv[0].astype(f32)
+        for i in range(GROUP):
+            pair_k[pl.ds(i, KVHALF, stride=GROUP), :] = pair[:KVHALF]
+            pair_v[pl.ds(i, KVHALF, stride=GROUP), :] = pair[KVHALF:]
+        score = jnp.sum(first_q[...].astype(f32) * pair_k[...], axis=1, keepdims=True) * SCALE
+        score = jnp.where(jnp.full((HALF // 2, 128), b, jnp.int32) == 0, paired(score), NEG)
+        values, level = merged(
+            [first_l[i] for i in range(nb)] + [score],
+            [first_o[i].astype(f32) for i in range(nb)] + [pair_v[...]],
+        )
+        row_o[0:HALF, :] = values
+        row_o[HALF:ROW_TILES, :] = level
+
     for t in order:
         peer = step(b, t)
         for cc in range(2):
@@ -270,39 +485,54 @@
                 row_o.at[row_at(peer * 2 + cc)], last.at[c * nb + b],
                 r2_send, r2_recv, role_dev(a, peer, cc),
             )
-    send(
-        row_o.at[row_at(b * 2 + 1 - c)], last.at[c * nb + b],
-        r2_send, r2_recv, dev(x, y, 1 - c),
-    )
+    send(row_o.at[row_at(b * 2 + 1 - c)], last.at[c * nb + b], r2_send, r2_recv, mate)
     last[c * nb + b] = row_o[row_at(b * 2 + c), :]
     await_bytes(last.at[0 : 2 * nb - 1], r2_recv)
 
-    live = jnp.full((HALF // 2, 128), me, jnp.int32) < len_s[0]
+    live = jnp.full((HALF, 128), me, jnp.int32) < len_s[0]
     for r in range(2):
-        levels = [last[r * nb + i, HALF:, :] for i in range(nb)]
-        top = functools.reduce(jnp.maximum, levels)
-        weights = [jnp.exp2(v - top) for v in levels]
-        inv = 1.0 / functools.reduce(jnp.add, weights)
-        outs = []
-        for k in range(2):
-            acc = None
-            for i in range(nb):
-                w = weights[i] * inv
-                term = w[:, k * 64 : k * 64 + 1] * last[
-                    r * nb + i, k * HALF // 2 : (k + 1) * HALF // 2, :
-                ]
-                acc = term if acc is None else acc + term
-            outs.append(jnp.where(live, acc, 0.0))
-        out_ref[r * HALF : (r + 1) * HALF, :] = jnp.concatenate(outs, axis=0).astype(bf16)
-
-    await_bytes(got_q.at[0 : rb - 1], s1_send)
-    await_bytes(got_kv.at[0 : rb - 1], s1_send)
+        got = [last[r * nb + i] for i in range(nb)]
+        values, _ = merged([v[HALF:] for v in got], [v[:HALF] for v in got])
+        out_ref[r * HALF : (r + 1) * HALF, :] = jnp.where(live, values, 0.0).astype(bf16)
+
+    @pl.when(rest & (x == 0))
+    def _():
+        await_bytes(got_q.at[0 : rb - 2], s1_send.at[0])
+
+    @pl.when(x > 0)
+    def _():
+        await_bytes(got_q.at[0 : rb - 1], s1_send.at[0])
+
+    await_bytes(got_kv.at[0 : rb - 1], s1_send.at[1])
     for i, buf in enumerate((keys, vals)):
         await_bytes(buf.at[c], ex_send.at[i])
-    await_bytes(all_q.at[:, 0 : (nb - 1) * rb, :], s2_send)
-    await_bytes(got_o.at[0 : nb - 1], r1_send)
-    await_bytes(got_l.at[0 : nb - 1], r1_send)
+    await_bytes(got_o.at[0 : nb - 1], r1_send.at[0])
+    await_bytes(got_l.at[0 : nb - 1], r1_send.at[1])
+
+    @pl.when(rest)
+    def _():
+        await_bytes(all_q.at[:, 0 : (nb - 1) * rb, :], s2_send)
+
+    @pl.when(a > 0)
+    def _():
+        await_bytes(first_o.at[a], back_send.at[0])
+        await_bytes(first_l.at[a], back_send.at[1])
+
+    @pl.when(me == stand)
+    def _():
+        await_bytes(mine_q, relay_send.at[0])
+
+    @pl.when(me == 1)
+    def _():
+        await_bytes(all_q.at[:, rb:, :], relay_send.at[1])
+        await_bytes(all_q, relay_send.at[2])
+
     await_bytes(last.at[0 : 2 * nb - 1], r2_send)
+
+    @pl.when(zero)
+    def _():
+        await_bytes(got_o.at[0 : nb - 1, :, 0:rb, :], first_send)
+        await_bytes(got_q.at[0 : rb - 1], first_send)
 
 
 def local(nb, q, kq, vq, k, v, lengths, offsets):
@@ -313,8 +543,8 @@
     dma = pltpu.SemaphoreType.DMA
     out = pl.pallas_call(
         functools.partial(kernel, nb),
-        out_shape=jax.ShapeDtypeStruct((H, HD), bf16),
-        in_specs=[pl.BlockSpec(memory_space=pl.ANY)] * 7,
+        out_shape=pltpu.VMEM((H, HD), bf16),
+        in_specs=[pl.BlockSpec(memory_space=pltpu.HBM)] * 7,
         out_specs=pl.BlockSpec(memory_space=pltpu.VMEM),
         scratch_shapes=[
             pltpu.VMEM((1, H * HD), bf16),
@@ -339,8 +569,15 @@
             pltpu.VMEM((nb, gs, 128), f32),
             pltpu.VMEM((rb * ROW_TILES, HD), f32),
             pltpu.VMEM((2 * nb, ROW_TILES, HD), f32),
-            dma((7,)), dma((2,)), dma((2,)), dma, dma((2,)), dma, dma((CHUNKS,)),
-            dma, dma((CHUNKS,)), dma, dma, dma,
+            pltpu.VMEM((HALF, rows, HD), bf16),
+            pltpu.VMEM((HALF, HD), bf16),
+            pltpu.VMEM((nb, HALF, HD), bf16),
+            pltpu.VMEM((nb, HALF // 2, HD), f32),
+            pltpu.VMEM((HALF, HD), f32),
+            pltpu.VMEM((HALF, HD), f32),
+            dma((7,)), dma((2,)), dma((2,)), dma((2,)), dma((2,)), dma, dma((CHUNKS,)),
+            dma((2,)), dma((CHUNKS,)), dma, dma, dma,
+            pltpu.SemaphoreType.REGULAR, dma((CHUNKS,)), dma((CHUNKS,)), dma((3,)), dma, dma, dma((2,)), dma((2,)),
         ],
         compiler_params=pltpu.CompilerParams(
             collective_id=0, has_side_effects=True, vmem_limit_bytes=56 * 1024 * 1024

time: 53.3 us -> 46.1 us (0.86)
  Pallas kernels: 50.4 us -> 44 us
  local copies, waits for them, and re-layouts: 1.32 us -> 0.62 us
    pallas_call x1, Pallas kernels: 50.4 us -> 44 us  [local(): pl.pallas_call(functools.partial(kernel, nb), out_shape=pltpu.VMEM((H, HD...]
    unnamed x1, local copies, waits for them, and re-layouts: 1.32 us -> 0.62 us
where the time goes in v2:
time: 46.1 us; the launch traced here: 46 us
  Pallas kernels  44 us (95%)
  between operations  1.3 us (3%)
  local copies, waits for them, and re-layouts  0.62 us (1%)
    pallas_call x1, Pallas kernels, local(): pl.pallas_call(functools.partial(kernel, nb), out_shape=pltpu.VMEM((H, HD...  44 us

profile of v2, /device:TPU:513, one launch (start us, length us, event | category | flops | bytes accessed | tf_op | source)
XLA Modules:
  0.0 46.0 jit_solution(9824914608038367752)
XLA Ops:
  1.3 44.0 %shard_map.73 = bf16[32,128]{1,0:T(8,128)(2,1)S(1)} custom-call(bf16[1,4096]{1,0:T(2,128)(2,1)} %q_hbm.1, bf16[1,2048]{1,0:T(2,128)(2,1)} %kq_hbm.1, bf16[1,2048]{1,0:T(2,128)(2,1)} %vq_hbm.1, bf16[512,2048]{1,0:T(8,128)(2,1)} %k_hbm.1, bf16[512,2048]{1,0:T(8,128)(2,1)} %v_hbm.1, s32[1]{0:T(128)S(6)} %copy.11.len_hbm, s32[1]{0:T(128)S(6)} %copy.12.off_hbm), custom_call_target="tpu_custom_call" | custom-call | tf_op jit(solution)/shard_map/pallas_call | solution.py:544
  45.3 0.6 %copy.10 = bf16[1,1,32,128]{3,1,2,0:T(2,128)(2,1)} copy(bf16[1,1,32,128]{3,2,1,0:T(8,128)(2,1)S(1)} %bitcast.5) | data formatting | bytes 16384

commit v3 on v2

--- a/solution.py
+++ b/solution.py
@@ -30,7 +30,7 @@
     out_ref,
     q_in, kq_in, vq_in, len_s, off_s, rows32, send_rows, got_q, got_kv, turn32,
     mine_q, all_q, keys, vals, parts, stats, own_o, own_l, got_o, got_l, row_o, last,
-    spare_q, first_q, first_o, first_l, pair_k, pair_v,
+    mate_q, spare_q, first_q, first_o, first_l, pair_k, pair_v,
     loc, ex_send, ex_recv, s1_send, s1_recv, s2_send, s2_recv,
     r1_send, r1_recv, st_recv, r2_send, r2_recv,
     here, spare_recv, relay_recv, relay_send, first_send, first_recv, back_send, back_recv,
@@ -60,7 +60,6 @@
 
     zero = me == 0
     rest = me > 0
-    stand = dev(0, 1, 0)
     order = sorted(range(1, nb), key=lambda t: -min(t, nb - t))
 
     def send(src, dst, ssem, rsem, target):
@@ -108,10 +107,6 @@
                 signal(barrier, dev(x, step(y, t), cc))
         signal(barrier, dev(x, y, 1 - c))
 
-    @pl.when((x > 0) & (y > 0))
-    def _():
-        signal(barrier, 0)
-
     for copy in small:
         copy.wait()
     for h in range(H):
@@ -135,9 +130,14 @@
     def _():
         got_q[0] = jnp.zeros((HALF, HD), bf16)
 
+    @pl.when(me == 1)
+    def _():
+        mate_q[0] = jnp.zeros((HALF, HD), bf16)
+        mate_q[1] = send_rows[0, 0]
+
     line = 4 * (nb - 1) + 1
     near = jnp.where((x == 0) | (y == 0), 1, 0)
-    pl.semaphore_wait(barrier, jnp.where(zero, 2 * nb * nb - 1, line - near))
+    pl.semaphore_wait(barrier, jnp.where(zero, line, line - near))
 
     @pl.when(zero)
     def _():
@@ -147,14 +147,12 @@
                 signal(here, dev(t, 0, cc))
         send_keys()
         first_q[...] = send_rows[0, 0]
-        far = sorted(
-            ((xx, yy) for xx in range(nb) for yy in range(nb)),
-            key=lambda p: -min(p[0], nb - p[0]) - min(p[1], nb - p[1]),
-        )
-        for xx, yy in far:
+        for t in order:
             for cc in range(2):
-                if xx or yy or cc:
-                    send(send_rows.at[cc, 0], first_q, first_send, first_recv, dev(xx, yy, cc))
+                send(send_rows.at[cc, 0], first_q, first_send, first_recv, dev(t, 0, cc))
+        send(send_rows.at[1, 0], first_q, first_send, first_recv, 1)
+        for t in order:
+            send(send_rows.at[0, 0], first_q, first_send, first_recv, dev(0, t, 0))
 
     my_block = pl.ds(pl.multiple_of(a * rb, rb), rb)
     per = HALF // CHUNKS
@@ -170,6 +168,10 @@
             @pl.when(to_0 > 0)
             def _(to_0=to_0):
                 send(send_rows.at[0, 0], got_q.at[y * 2 + c], s1_send.at[0], s1_recv.at[0], to_0)
+
+            @pl.when(to_0 == 0)
+            def _():
+                send(send_rows.at[0, 0], mate_q.at[y * 2 + c], s1_send.at[0], relay_recv, 1)
 
             send(
                 send_rows.at[1, 0], got_q.at[x * 2 + c], s1_send.at[0], s1_recv.at[0],
@@ -219,15 +221,24 @@
             block = turn32[pl.ds(h, rb, stride=HALF), :].astype(bf16)
             mine_q[h] = block
             all_q[h, my_block, :] = block
+
+        @pl.when(me == 1)
+        def _():
+            await_bytes(mate_q.at[2:rb], relay_recv)
+            for i in range(rb):
+                turn32[i * HALF : (i + 1) * HALF, :] = mate_q[i].astype(f32)
+            for h in range(HALF):
+                spare_q[h, 0:rb, :] = turn32[pl.ds(h, rb, stride=HALF), :].astype(bf16)
+            for j in range(CHUNKS):
+                some = pl.ds(j * per, per)
+                for t in order:
+                    send(
+                        spare_q.at[some, 0:rb, :], all_q.at[some, 0:rb, :],
+                        relay_send.at[0], s2_recv.at[j], dev(t, 0, 0),
+                    )
+
         for j in range(CHUNKS):
             some = pl.ds(j * per, per)
-
-            @pl.when(me == stand)
-            def _(some=some, j=j):
-                send(
-                    mine_q.at[some], spare_q.at[some, my_block, :],
-                    relay_send.at[0], relay_recv.at[j], 1,
-                )
 
             for t in order:
                 target = role_dev(step(a, t), b, c)
@@ -254,18 +265,14 @@
         def _():
             send_keys()
             send_mate_row(1, got_kv.at[b * 2 + c])
-            for j in range(CHUNKS):
-                block = spare_q.at[pl.ds(j * per, per), 0:rb, :]
-                await_bytes(block, relay_recv.at[j])
-                for t in order:
-                    send(
-                        block, all_q.at[pl.ds(j * per, per), 0:rb, :],
-                        relay_send.at[1], s2_recv.at[j], dev(t, 0, 0),
-                    )
 
         @pl.when(me > 1)
         def _():
             send_row_0(0)
+
+        await_bytes(first_q, first_recv)
+        for t in order:
+            send(first_q, first_q, first_send, first_recv, dev(x, t, c))
 
     lane = lax.broadcasted_iota(jnp.int32, (gs, 128), 1)
     for i in range(nb):
@@ -286,7 +293,7 @@
         def _():
             some = pl.ds(first, per)
             await_bytes(spare_q.at[some, rb:, :], spare_recv.at[j])
-            send(spare_q.at[some], all_q.at[some], relay_send.at[2], s2_recv.at[j], 0)
+            send(spare_q.at[some], all_q.at[some], relay_send.at[1], s2_recv.at[j], 0)
 
         @pl.when(zero)
         def _():
@@ -336,43 +343,15 @@
                 got_o.at[a, pl.ds(first, per)],
                 r1_send.at[0], r1_recv.at[j], role_dev(peer, b, c),
             )
+
+            @pl.when(j == CHUNKS - 1)
+            def _(peer=peer):
+                send(stats.at[peer], got_l.at[a], r1_send.at[1], st_recv, role_dev(peer, b, c))
+
         return carry
 
     lax.fori_loop(0, CHUNKS, chunk, 0)
-    for t in order:
-        peer = step(a, t)
-        send(stats.at[peer], got_l.at[a], r1_send.at[1], st_recv, role_dev(peer, b, c))
-
-    await_bytes(got_kv.at[0 : rb - 1], s1_recv.at[1])
-    for i in range(rb):
-        turn32[i * HALF : (i + 1) * HALF, :] = got_kv[i].astype(f32)
-
-    def row_of(aa, bb, cc):
-        return dev(aa * (1 - c) + bb * c, bb * (1 - c) + aa * c, cc)
-
-    spot = lax.rem(lax.broadcasted_iota(jnp.int32, (GROUP * rb, rb), 0), rb)
-    key_spot = lax.broadcasted_iota(jnp.int32, (GROUP * rb, rb), 1)
-    see = row_of(key_spot // 2, b, lax.rem(key_spot, 2)) <= row_of(a, spot // 2, lax.rem(spot, 2))
-    own = jnp.full((gs, 128), NEG, f32)
-    for g in range(KVHALF):
-        key = turn32[pl.ds(g, rb, stride=HALF), :].astype(bf16)
-        val = turn32[pl.ds(KVHALF + g, rb, stride=HALF), :].astype(bf16)
-        q = all_q[g * GROUP : (g + 1) * GROUP, my_block, :].reshape(GROUP * rb, HD)
-        s = lax.dot_general(q, key, (((1,), (1,)), ((), ())), preferred_element_type=f32)
-        s = jnp.where(see, s, NEG)
-        top = jnp.max(s, axis=1, keepdims=True)
-        p = jnp.exp2((s - top) * SCALE).astype(bf16)
-        den = jnp.sum(p.astype(f32), axis=1, keepdims=True)
-        num = jnp.dot(p, val, preferred_element_type=f32)
-        own_o[g * GROUP : (g + 1) * GROUP] = (num / den).reshape(GROUP, rb, HD)
-        level = top * SCALE + jnp.log2(den)
-        for i in range(GROUP):
-            for k in range(groups):
-                at = i * rb + k * gs
-                own = jnp.where(lane == k * HALF + g * GROUP + i, level[at : at + gs], own)
-    own_l[...] = own
-
-    @pl.when(rest)
+    @pl.when(y > 0)
     def _():
         await_bytes(first_q, first_recv)
 
@@ -412,6 +391,35 @@
         target = role_dev(0, b, c)
         send(first_o.at[a], first_o.at[a], back_send.at[0], back_recv.at[0], target)
         send(first_l.at[a], first_l.at[a], back_send.at[1], back_recv.at[1], target)
+
+    await_bytes(got_kv.at[0 : rb - 1], s1_recv.at[1])
+    for i in range(rb):
+        turn32[i * HALF : (i + 1) * HALF, :] = got_kv[i].astype(f32)
+
+    def row_of(aa, bb, cc):
+        return dev(aa * (1 - c) + bb * c, bb * (1 - c) + aa * c, cc)
+
+    spot = lax.rem(lax.broadcasted_iota(jnp.int32, (GROUP * rb, rb), 0), rb)
+    key_spot = lax.broadcasted_iota(jnp.int32, (GROUP * rb, rb), 1)
+    see = row_of(key_spot // 2, b, lax.rem(key_spot, 2)) <= row_of(a, spot // 2, lax.rem(spot, 2))
+    own = jnp.full((gs, 128), NEG, f32)
+    for g in range(KVHALF):
+        key = turn32[pl.ds(g, rb, stride=HALF), :].astype(bf16)
+        val = turn32[pl.ds(KVHALF + g, rb, stride=HALF), :].astype(bf16)
+        q = all_q[g * GROUP : (g + 1) * GROUP, my_block, :].reshape(GROUP * rb, HD)
+        s = lax.dot_general(q, key, (((1,), (1,)), ((), ())), preferred_element_type=f32)
+        s = jnp.where(see, s, NEG)
+        top = jnp.max(s, axis=1, keepdims=True)
+        p = jnp.exp2((s - top) * SCALE).astype(bf16)
+        den = jnp.sum(p.astype(f32), axis=1, keepdims=True)
+        num = jnp.dot(p, val, preferred_element_type=f32)
+        own_o[g * GROUP : (g + 1) * GROUP] = (num / den).reshape(GROUP, rb, HD)
+        level = top * SCALE + jnp.log2(den)
+        for i in range(GROUP):
+            for k in range(groups):
+                at = i * rb + k * gs
+                own = jnp.where(lane == k * HALF + g * GROUP + i, level[at : at + gs], own)
+    own_l[...] = own
 
     await_bytes(got_l.at[0 : nb - 1], st_recv)
     levels = [stats[a]] + [got_l[step(a, t)] for t in range(1, nb)] + [own_l[...]]
@@ -461,6 +469,22 @@
             outs.append(functools.reduce(jnp.add, terms))
         return jnp.concatenate(outs, axis=0), top + jnp.log2(total)
 
+    mine_last = last.at[c * nb + b]
+    for t in order:
+        peer = step(b, t)
+        for cc in range(2):
+            target = role_dev(a, peer, cc)
+
+            @pl.when(target > 0)
+            def _(row=peer * 2 + cc, target=target):
+                send(row_o.at[row_at(row)], mine_last, r2_send, r2_recv, target)
+
+    @pl.when(me != 1)
+    def _():
+        send(row_o.at[row_at(b * 2 + 1 - c)], mine_last, r2_send, r2_recv, mate)
+
+    mine_last[...] = row_o[row_at(b * 2 + c), :]
+
     @pl.when(a == 0)
     def _():
         await_bytes(first_o.at[0 : nb - 1], back_recv.at[0])
@@ -478,15 +502,14 @@
         row_o[0:HALF, :] = values
         row_o[HALF:ROW_TILES, :] = level
 
-    for t in order:
-        peer = step(b, t)
-        for cc in range(2):
-            send(
-                row_o.at[row_at(peer * 2 + cc)], last.at[c * nb + b],
-                r2_send, r2_recv, role_dev(a, peer, cc),
-            )
-    send(row_o.at[row_at(b * 2 + 1 - c)], last.at[c * nb + b], r2_send, r2_recv, mate)
-    last[c * nb + b] = row_o[row_at(b * 2 + c), :]
+        @pl.when(zero)
+        def _():
+            mine_last[...] = row_o[0:ROW_TILES, :]
+
+        @pl.when(rest)
+        def _():
+            send(row_o.at[0:ROW_TILES], mine_last, r2_send, r2_recv, 0)
+
     await_bytes(last.at[0 : 2 * nb - 1], r2_recv)
 
     live = jnp.full((HALF, 128), me, jnp.int32) < len_s[0]
@@ -495,11 +518,11 @@
         values, _ = merged([v[HALF:] for v in got], [v[:HALF] for v in got])
         out_ref[r * HALF : (r + 1) * HALF, :] = jnp.where(live, values, 0.0).astype(bf16)
 
-    @pl.when(rest & (x == 0))
+    @pl.when(me == 1)
     def _():
         await_bytes(got_q.at[0 : rb - 2], s1_send.at[0])
 
-    @pl.when(x > 0)
+    @pl.when(me > 1)
     def _():
         await_bytes(got_q.at[0 : rb - 1], s1_send.at[0])
 
@@ -518,21 +541,20 @@
         await_bytes(first_o.at[a], back_send.at[0])
         await_bytes(first_l.at[a], back_send.at[1])
 
-    @pl.when(me == stand)
-    def _():
-        await_bytes(mine_q, relay_send.at[0])
-
     @pl.when(me == 1)
     def _():
-        await_bytes(all_q.at[:, rb:, :], relay_send.at[1])
-        await_bytes(all_q, relay_send.at[2])
+        await_bytes(all_q.at[:, rb:, :], relay_send.at[0])
+        await_bytes(all_q, relay_send.at[1])
 
     await_bytes(last.at[0 : 2 * nb - 1], r2_send)
 
     @pl.when(zero)
     def _():
-        await_bytes(got_o.at[0 : nb - 1, :, 0:rb, :], first_send)
         await_bytes(got_q.at[0 : rb - 1], first_send)
+
+    @pl.when(y == 0)
+    def _():
+        await_bytes(got_q.at[0 : nb - 1], first_send)
 
 
 def local(nb, q, kq, vq, k, v, lengths, offsets):
@@ -569,6 +591,7 @@
             pltpu.VMEM((nb, gs, 128), f32),
             pltpu.VMEM((rb * ROW_TILES, HD), f32),
             pltpu.VMEM((2 * nb, ROW_TILES, HD), f32),
+            pltpu.VMEM((rb, HALF, HD), bf16),
             pltpu.VMEM((HALF, rows, HD), bf16),
             pltpu.VMEM((HALF, HD), bf16),
             pltpu.VMEM((nb, HALF, HD), bf16),
@@ -577,7 +600,7 @@
             pltpu.VMEM((HALF, HD), f32),
             dma((7,)), dma((2,)), dma((2,)), dma((2,)), dma((2,)), dma, dma((CHUNKS,)),
             dma((2,)), dma((CHUNKS,)), dma, dma, dma,
-            pltpu.SemaphoreType.REGULAR, dma((CHUNKS,)), dma((CHUNKS,)), dma((3,)), dma, dma, dma((2,)), dma((2,)),
+            pltpu.SemaphoreType.REGULAR, dma((CHUNKS,)), dma, dma((2,)), dma, dma, dma((2,)), dma((2,)),
         ],
         compiler_params=pltpu.CompilerParams(
             collective_id=0, has_side_effects=True, vmem_limit_bytes=56 * 1024 * 1024

time: 46.1 us -> 45.2 us (0.980)
  Pallas kernels: 44 us -> 43.1 us
    pallas_call x1, Pallas kernels: 44 us -> 43.1 us  [local(): pl.pallas_call(functools.partial(kernel, nb), out_shape=pltpu.VMEM((H, HD...]
where the time goes in v3:
time: 45.2 us; the launch traced here: 45 us
  Pallas kernels  43.1 us (95%)
  between operations  1.3 us (3%)
  local copies, waits for them, and re-layouts  0.62 us (1%)
    pallas_call x1, Pallas kernels, local(): pl.pallas_call(functools.partial(kernel, nb), out_shape=pltpu.VMEM((H, HD...  43.1 us

profile of v3, /device:TPU:513, one launch (start us, length us, event | category | flops | bytes accessed | tf_op | source)
XLA Modules:
  0.0 45.0 jit_solution(14914223192012896274)
XLA Ops:
  1.3 43.1 %shard_map.73 = bf16[32,128]{1,0:T(8,128)(2,1)S(1)} custom-call(bf16[1,4096]{1,0:T(2,128)(2,1)} %q_hbm.1, bf16[1,2048]{1,0:T(2,128)(2,1)} %kq_hbm.1, bf16[1,2048]{1,0:T(2,128)(2,1)} %vq_hbm.1, bf16[512,2048]{1,0:T(8,128)(2,1)} %k_hbm.1, bf16[512,2048]{1,0:T(8,128)(2,1)} %v_hbm.1, s32[1]{0:T(128)S(6)} %copy.11.len_hbm, s32[1]{0:T(128)S(6)} %copy.12.off_hbm), custom_call_target="tpu_custom_call" | custom-call | tf_op jit(solution)/shard_map/pallas_call | solution.py:566
  44.4 0.6 %copy.10 = bf16[1,1,32,128]{3,1,2,0:T(2,128)(2,1)} copy(bf16[1,1,32,128]{3,2,1,0:T(8,128)(2,1)S(1)} %bitcast.5) | data formatting | bytes 16384

commit v4 on v3

--- a/solution.py
+++ b/solution.py
@@ -84,7 +84,7 @@
         pltpu.make_async_copy(k_hbm.at[:, mine], keys.at[c], loc.at[5]),
         pltpu.make_async_copy(v_hbm.at[:, mine], vals.at[c], loc.at[6]),
     ]
-    for copy in small + large:
+    for copy in small:
         copy.start()
     mate = dev(x, y, 1 - c)
 
@@ -107,6 +107,8 @@
                 signal(barrier, dev(x, step(y, t), cc))
         signal(barrier, dev(x, y, 1 - c))
 
+    for copy in large:
+        copy.start()
     for copy in small:
         copy.wait()
     for h in range(H):

time: 45.2 us -> 45.2 us (level)
  no operation moved by 1% of the time
where the time goes in v4:
time: 45.2 us; the launch traced here: 45 us
  Pallas kernels  43.1 us (95%)
  between operations  1.3 us (3%)
  local copies, waits for them, and re-layouts  0.62 us (1%)
    pallas_call x1, Pallas kernels, local(): pl.pallas_call(functools.partial(kernel, nb), out_shape=pltpu.VMEM((H, HD...  43.1 us

profile of v4, /device:TPU:513, one launch (start us, length us, event | category | flops | bytes accessed | tf_op | source)
XLA Modules:
  0.0 45.0 jit_solution(16378440816418804504)
XLA Ops:
  1.3 43.1 %shard_map.73 = bf16[32,128]{1,0:T(8,128)(2,1)S(1)} custom-call(bf16[1,4096]{1,0:T(2,128)(2,1)} %q_hbm.1, bf16[1,2048]{1,0:T(2,128)(2,1)} %kq_hbm.1, bf16[1,2048]{1,0:T(2,128)(2,1)} %vq_hbm.1, bf16[512,2048]{1,0:T(8,128)(2,1)} %k_hbm.1, bf16[512,2048]{1,0:T(8,128)(2,1)} %v_hbm.1, s32[1]{0:T(128)S(6)} %copy.11.len_hbm, s32[1]{0:T(128)S(6)} %copy.12.off_hbm), custom_call_target="tpu_custom_call" | custom-call | tf_op jit(solution)/shard_map/pallas_call | solution.py:568
  44.4 0.6 %copy.10 = bf16[1,1,32,128]{3,1,2,0:T(2,128)(2,1)} copy(bf16[1,1,32,128]{3,2,1,0:T(8,128)(2,1)S(1)} %bitcast.5) | data formatting | bytes 16384

commit v5 on v4

--- a/solution.py
+++ b/solution.py
@@ -156,6 +156,7 @@
         for t in order:
             send(send_rows.at[0, 0], first_q, first_send, first_recv, dev(0, t, 0))
 
+    line_peers = [(step(a, t), role_dev(step(a, t), b, c)) for t in order]
     my_block = pl.ds(pl.multiple_of(a * rb, rb), rb)
     per = HALF // CHUNKS
 
@@ -219,32 +220,47 @@
 
         for i in range(rb):
             turn32[i * HALF : (i + 1) * HALF, :] = got_q[i].astype(f32)
-        for h in range(HALF):
-            block = turn32[pl.ds(h, rb, stride=HALF), :].astype(bf16)
-            mine_q[h] = block
-            all_q[h, my_block, :] = block
-
-        @pl.when(me == 1)
-        def _():
-            await_bytes(mate_q.at[2:rb], relay_recv)
-            for i in range(rb):
-                turn32[i * HALF : (i + 1) * HALF, :] = mate_q[i].astype(f32)
-            for h in range(HALF):
-                spare_q[h, 0:rb, :] = turn32[pl.ds(h, rb, stride=HALF), :].astype(bf16)
-            for j in range(CHUNKS):
-                some = pl.ds(j * per, per)
-                for t in order:
-                    send(
-                        spare_q.at[some, 0:rb, :], all_q.at[some, 0:rb, :],
-                        relay_send.at[0], s2_recv.at[j], dev(t, 0, 0),
-                    )
-
+
+    def turn(h):
+        block = turn32[pl.ds(h, rb, stride=HALF), :].astype(bf16)
+        mine_q[h] = block
+        all_q[h, my_block, :] = block
+
+    @pl.when((y > 0) | (me > 1) & (c == 1))
+    def _():
         for j in range(CHUNKS):
             some = pl.ds(j * per, per)
-
+            for h in range(j * per, (j + 1) * per):
+                turn(h)
+            for _, target in line_peers:
+                send(mine_q.at[some], all_q.at[some, my_block, :], s2_send, s2_recv.at[j], target)
+
+    @pl.when(me == 1)
+    def _():
+        for h in range(HALF):
+            turn(h)
+        await_bytes(mate_q.at[2:rb], relay_recv)
+        for i in range(rb):
+            turn32[i * HALF : (i + 1) * HALF, :] = mate_q[i].astype(f32)
+        for h in range(HALF):
+            spare_q[h, 0:rb, :] = turn32[pl.ds(h, rb, stride=HALF), :].astype(bf16)
+        for j in range(CHUNKS):
+            some = pl.ds(j * per, per)
             for t in order:
-                target = role_dev(step(a, t), b, c)
-
+                send(
+                    spare_q.at[some, 0:rb, :], all_q.at[some, 0:rb, :],
+                    relay_send.at[0], s2_recv.at[j], dev(t, 0, 0),
+                )
+            for _, target in line_peers:
+                send(mine_q.at[some], all_q.at[some, my_block, :], s2_send, s2_recv.at[j], target)
+
+    @pl.when((y == 0) & (c == 0) & rest)
+    def _():
+        for h in range(HALF):
+            turn(h)
+        for j in range(CHUNKS):
+            some = pl.ds(j * per, per)
+            for _, target in line_peers:
                 @pl.when(target > 0)
                 def _(some=some, target=target, j=j):
                     send(
@@ -338,17 +354,16 @@
                         at = z * rows + i * rb + k * gs
                         tile = jnp.where(lane == k * HALF + head + z, level[at : at + gs], tile)
                 stats[i] = tile
-        for t in order:
-            peer = step(a, t)
+        for peer, target in line_peers:
             send(
                 parts.at[pl.ds(first, per), pl.ds(pl.multiple_of(peer * rb, rb), rb), :],
                 got_o.at[a, pl.ds(first, per)],
-                r1_send.at[0], r1_recv.at[j], role_dev(peer, b, c),
+                r1_send.at[0], r1_recv.at[j], target,
             )
 
             @pl.when(j == CHUNKS - 1)
-            def _(peer=peer):
-                send(stats.at[peer], got_l.at[a], r1_send.at[1], st_recv, role_dev(peer, b, c))
+            def _(peer=peer, target=target):
+                send(stats.at[peer], got_l.at[a], r1_send.at[1], st_recv, target)
 
         return carry
 

time: 45.2 us -> 45.1 us (level)
  no operation moved by 1% of the time
where the time goes in v5:
time: 45.1 us; the launch traced here: 44.9 us
  Pallas kernels  43 us (95%)
  between operations  1.3 us (3%)
  local copies, waits for them, and re-layouts  0.62 us (1%)
    pallas_call x1, Pallas kernels, local(): pl.pallas_call(functools.partial(kernel, nb), out_shape=pltpu.VMEM((H, HD...  43 us

profile of v5, /device:TPU:513, one launch (start us, length us, event | category | flops | bytes accessed | tf_op | source)
XLA Modules:
  0.0 44.9 jit_solution(4093471112034823394)
XLA Ops:
  1.3 43.0 %shard_map.73 = bf16[32,128]{1,0:T(8,128)(2,1)S(1)} custom-call(bf16[1,4096]{1,0:T(2,128)(2,1)} %q_hbm.1, bf16[1,2048]{1,0:T(2,128)(2,1)} %kq_hbm.1, bf16[1,2048]{1,0:T(2,128)(2,1)} %vq_hbm.1, bf16[512,2048]{1,0:T(8,128)(2,1)} %k_hbm.1, bf16[512,2048]{1,0:T(8,128)(2,1)} %v_hbm.1, s32[1]{0:T(128)S(6)} %copy.11.len_hbm, s32[1]{0:T(128)S(6)} %copy.12.off_hbm), custom_call_target="tpu_custom_call" | custom-call | tf_op jit(solution)/shard_map/pallas_call | solution.py:583
  44.3 0.6 %copy.10 = bf16[1,1,32,128]{3,1,2,0:T(2,128)(2,1)} copy(bf16[1,1,32,128]{3,2,1,0:T(8,128)(2,1)S(1)} %bitcast.5) | data formatting | bytes 16384
